TPU v7x, 32 devices: a whole 2x2x4 slice. The times are simulated.
32 devices in a mesh: pp: 2 (over y), cp: 8 (over z, x), tp: 2 (over core).
Axes of the slice: x: 2, y: 2, z: 4, core: 2. Of those that a mesh axis runs over, the one named last changes fastest.
Arguments:
- queries: bfloat16 [2, 1024, 4096], P('pp', 'cp', 'tp'), may hold values from -4.5 to 4.5
- keys: bfloat16 [2, 1024, 256], P('pp', 'cp', 'tp'), may hold values from -4.5 to 4.5
- values: bfloat16 [2, 1024, 256], P('pp', 'cp', 'tp'), may hold values from -6 to 6
- out_weight: bfloat16 [4096, 16384], P('tp', 'cp'), may hold values from -1.5 to 1.5
- span_order: int32 [16], replicated, may hold values from 0 to 15, as said below
Outputs:
- handed: bfloat16 [2, 8, 128, 16384], P('pp', None, 'tp', 'cp')
Inputs may be any that keep to these rules, and one draw needn't show every extreme that they name: `span_order`: the two stored blocks 2r and 2r + 1 are the sequence blocks j and 15 - j for some j, in either order; every sequence block appears once.
All inputs are finite; a program needn't handle non-finite values.
Results may differ from a plain program's by a relative error of at most 0.0095.
Values may be sent and summed in bfloat16 or wider, within the bound.
A program may use at most 128 MiB of HBM per device.

v0:
```python
import functools

import jax
import jax.numpy as jnp
from jax import lax
from jax.experimental import pallas as pl
from jax.experimental.pallas import tpu as pltpu
from jax.sharding import PartitionSpec as P

HEAD = 128
PARTS = 4
MESH = pl.DeviceIdType.MESH


def kernel(
    n_pp,
    n_cp,
    order_ref,
    q_ref,
    k_ref,
    v_ref,
    w_ref,
    out_ref,
    kv,
    qb,
    ga,
    wb,
    own,
    part,
    give,
    take,
    ob,
    mask,
    w_sem,
    out_sem,
    ys_sem,
    yr_sem,
    kvz_sem,
    kvx_sem,
    kvr_sem,
    up_sem,
    down_sem,
    x_sem,
    g_sem,
    ts_sem,
    tr_sem,
):
    pp, cp, tp = lax.axis_index("pp"), lax.axis_index("cp"), lax.axis_index("tp")
    line = n_cp // 2
    i, x = cp // 2, cp % 2
    rows = q_ref.shape[1]
    half = rows // 2
    width = qb.shape[2]
    tile = give.shape[3]
    heads = width // HEAD
    after, before = lax.rem(pp + 1, n_pp), lax.rem(pp + n_pp - 1, n_pp)
    right = (pp, i * 2 + 1 - x, tp)
    sibling = (pp, cp, 1 - tp)

    def remote(src, dst, send, recv, device):
        return pltpu.make_async_remote_copy(
            src_ref=src,
            dst_ref=dst,
            send_sem=send,
            recv_sem=recv,
            device_id=device,
            device_id_type=MESH,
        )

    load_w = pltpu.make_async_copy(w_ref, wb, w_sem)
    load_w.start()

    barrier = pltpu.get_barrier_semaphore()
    for device in ((after, cp, tp), (before, cp, tp), right, sibling):
        pl.semaphore_signal(barrier, inc=1, device_id=device, device_id_type=MESH)

    @pl.loop(0, line)
    def _(j):
        @pl.when(j != i)
        def _():
            pl.semaphore_signal(
                barrier, inc=1, device_id=(pp, j * 2 + x, tp), device_id_type=MESH
            )

    pl.semaphore_wait(barrier, 3 + line)

    shift = [
        remote(k_ref.at[0], kv.at[cp, 0], ys_sem.at[0], yr_sem.at[0], (after, cp, tp)),
        remote(v_ref.at[0], kv.at[cp, 1], ys_sem.at[1], yr_sem.at[1], (after, cp, tp)),
    ]
    for s in range(PARTS):
        shift.append(
            remote(
                q_ref.at[0, :, pl.ds(s * width, width)],
                qb.at[s],
                ys_sem.at[2 + s],
                yr_sem.at[2 + s],
                (after, cp, tp),
            )
        )
    for copy in shift:
        copy.start()
    shift[0].wait_recv()
    shift[1].wait_recv()

    def kv_line(c, j):
        return remote(kv.at[c], kv.at[c], kvz_sem.at[j], kvr_sem.at[c], (pp, j * 2 + x, tp))

    def kv_side(c):
        return remote(kv.at[c], kv.at[c], kvx_sem.at[c // 2], kvr_sem.at[c], right)

    def around(body):
        @pl.loop(1, line)
        def _(d):
            for j, inside in ((i - d, i - d >= 0), (i + d, i + d < line)):

                @pl.when(inside)
                def _():
                    body(j)

    around(lambda j: kv_line(cp, j).start())
    kv_side(cp).start()

    def pass_kv(j):
        kv_side(j * 2 + x).wait_recv()
        kv_side(j * 2 + x).start()

    around(pass_kv)

    @pl.loop(0, line)
    def _(j):
        kv_side(j * 2 + 1 - x).wait_recv()

    row = lax.broadcasted_iota(jnp.int32, (rows, 1), 0)
    query_pos = jnp.where(row < half, order_ref[2 * cp] * half, order_ref[2 * cp + 1] * half - half) + row
    for c in range(n_cp):
        col = lax.broadcasted_iota(jnp.int32, (1, rows), 1)
        key_pos = jnp.where(col < half, order_ref[2 * c] * half, order_ref[2 * c + 1] * half - half) + col
        mask[:, c * rows : (c + 1) * rows] = jnp.where(key_pos <= query_pos, 0.0, -1e30)

    def send_up(c, s):
        return remote(
            ga.at[c, s], ga.at[c, s], up_sem.at[c // 2, s], g_sem.at[c, s], (pp, cp + 2, tp)
        )

    def send_down(c, s):
        return remote(
            ga.at[c, s], ga.at[c, s], down_sem.at[c // 2, s], g_sem.at[c, s], (pp, cp - 2, tp)
        )

    def send_side(c, s):
        return remote(ga.at[c, s], ga.at[c, s], x_sem.at[c // 2, s], g_sem.at[c, s], right)

    scale = HEAD ** (-0.5)
    length = n_cp * rows
    for s in range(PARTS):
        shift[2 + s].wait_recv()

        @pl.loop(0, heads)
        def _(h):
            at = pl.ds(pl.multiple_of(h * HEAD, HEAD), HEAD)
            keys = kv[:, 0].reshape(length, HEAD)
            values = kv[:, 1].reshape(length, HEAD)
            score = lax.dot_general(
                qb[s, :, at], keys, (((1,), (1,)), ((), ())), preferred_element_type=jnp.float32
            )
            score = score * scale + mask[...]
            weight = jnp.exp(score - jnp.max(score, axis=1, keepdims=True))
            total = jnp.sum(weight, axis=1, keepdims=True)
            mixed = jnp.dot(weight.astype(jnp.bfloat16), values, preferred_element_type=jnp.float32)
            ga[cp, s, :, at] = (mixed / total).astype(jnp.bfloat16)

        @pl.when(i + 1 < line)
        def _():
            send_up(cp, s).start()

        @pl.when(i > 0)
        def _():
            send_down(cp, s).start()

        send_side(cp, s).start()

    load_w.wait()

    def swap(c, n):
        return remote(give.at[c, n], take.at[c, n], ts_sem.at[c, n], tr_sem.at[c, n], sibling)

    def columns(n):
        return pl.ds(pl.multiple_of(n * tile, tile), tile)

    def project(c, n):
        total = None
        for s in range(PARTS):
            term = jnp.dot(
                ga[c, s],
                wb[s * width : (s + 1) * width, columns(n)],
                preferred_element_type=jnp.float32,
            )
            total = term if total is None else total + term
        part[...] = total
        give[c, n] = part[pl.ds(pl.multiple_of((1 - tp) * half, half), half), :].astype(jnp.bfloat16)
        own[c, n] = part[pl.ds(pl.multiple_of(tp * half, half), half), :]
        swap(c, n).start()

    def finish(c, n):
        swap(c, n).wait_recv()
        ob[c, :, columns(n)] = (own[c, n] + take[c, n].astype(jnp.float32)).astype(jnp.bfloat16)

    def store(c):
        return pltpu.make_async_copy(ob.at[c], out_ref.at[0, c], out_sem.at[c])

    @pl.loop(PARTS, (line + 3) * PARTS)
    def _(step):
        d, s = step // PARTS, step % PARTS

        @pl.when((d < line) & (i - d >= 0))
        def _():
            c = cp - 2 * d
            send_side(c, s).wait_recv()

            @pl.when(i + 1 < line)
            def _():
                send_up(c, s).start()

            send_side(c, s).start()

        @pl.when((d < line) & (i + d < line))
        def _():
            c = cp + 2 * d
            send_side(c, s).wait_recv()

            @pl.when(i > 0)
            def _():
                send_down(c, s).start()

            send_side(c, s).start()

        @pl.loop(0, 4)
        def _(k):
            side = k // 2
            sign = 1 - 2 * (k % 2)

            def item(lag):
                far = d - lag - side
                j = i + sign * far
                c = j * 2 + (x + side) % 2
                fine = (far >= 0) & (far < line) & (j >= 0) & (j < line)
                return c, fine & ((far > 0) | (sign > 0))

            c, fine = item(1)

            @pl.when(fine)
            def _():
                @pl.when((side == 1) & (s == 0))
                def _():
                    for r in range(PARTS):
                        send_side(c, r).wait_recv()

                project(c, s)

            e, done = item(2)

            @pl.when(done)
            def _():
                finish(e, s)

                @pl.when(s == PARTS - 1)
                def _():
                    store(e).start()

    for copy in shift:
        copy.wait_send()
    around(lambda j: kv_line(cp, j).wait_send())

    @pl.loop(0, line)
    def _(j):
        c = j * 2 + x
        kv_side(c).wait_send()
        for s in range(PARTS):
            send_side(c, s).wait_send()

            @pl.when((j <= i) & (i + 1 < line))
            def _():
                send_up(c, s).wait_send()

            @pl.when((j >= i) & (i > 0))
            def _():
                send_down(c, s).wait_send()

    @pl.loop(0, n_cp)
    def _(c):
        for n in range(PARTS):
            swap(c, n).wait_send()
        store(c).wait()


def on_device(n_pp, n_cp, queries, keys, values, out_weight, span_order):
    rows = queries.shape[1]
    half = rows // 2
    depth, wide = out_weight.shape
    width, tile = depth // PARTS, wide // PARTS
    line = n_cp // 2
    vmem = pl.BlockSpec(memory_space=pltpu.VMEM)
    hbm = pl.BlockSpec(memory_space=pl.ANY)
    dma = pltpu.SemaphoreType.DMA
    return pl.pallas_call(
        functools.partial(kernel, n_pp, n_cp),
        out_shape=jax.ShapeDtypeStruct((1, n_cp, half, wide), jnp.bfloat16),
        in_specs=[pl.BlockSpec(memory_space=pltpu.SMEM), vmem, vmem, vmem, hbm],
        out_specs=hbm,
        scratch_shapes=[
            pltpu.VMEM((n_cp, 2, rows, HEAD), jnp.bfloat16),
            pltpu.VMEM((PARTS, rows, width), jnp.bfloat16),
            pltpu.VMEM((n_cp, PARTS, rows, width), jnp.bfloat16),
            pltpu.VMEM((depth, wide), jnp.bfloat16),
            pltpu.VMEM((n_cp, PARTS, half, tile), jnp.float32),
            pltpu.VMEM((rows, tile), jnp.float32),
            pltpu.VMEM((n_cp, PARTS, half, tile), jnp.bfloat16),
            pltpu.VMEM((n_cp, PARTS, half, tile), jnp.bfloat16),
            pltpu.VMEM((n_cp, half, wide), jnp.bfloat16),
            pltpu.VMEM((rows, n_cp * rows), jnp.float32),
            dma,
            dma((n_cp,)),
            dma((2 + PARTS,)),
            dma((2 + PARTS,)),
            dma((line,)),
            dma((line,)),
            dma((n_cp,)),
            dma((line, PARTS)),
            dma((line, PARTS)),
            dma((line, PARTS)),
            dma((n_cp, PARTS)),
            dma((n_cp, PARTS)),
            dma((n_cp, PARTS)),
        ],
        compiler_params=pltpu.CompilerParams(
            collective_id=0, has_side_effects=True, vmem_limit_bytes=60000 * 1024
        ),
    )(span_order, queries, keys, values, out_weight)


def solution(mesh):
    placed = (P("pp", "cp", "tp"), P("pp", "cp", "tp"), P("pp", "cp", "tp"), P("tp", "cp"), P())
    return jax.shard_map(
        functools.partial(on_device, mesh.shape["pp"], mesh.shape["cp"]),
        mesh=mesh,
        in_specs=placed,
        out_specs=P("pp", None, "tp", "cp"),
        check_vma=False,
    )
```

profile of v0, /device:TPU:1, one launch (start us, length us, event | category | flops | bytes accessed | tf_op | source)
XLA Modules:
  0.0 75.0 jit_solution(1995090452562951668)
XLA Ops:
  0.0 71.8 %shard_map.55 = bf16[1,8,64,2048]{3,2,1,0:T(8,128)(2,1)} custom-call(s32[16]{0:T(128)} %order_ref.1, bf16[1,128,2048]{2,1,0:T(8,128)(2,1)} %q_ref.1, bf16[1,128,128]{2,1,0:T(8,128)(2,1)} %k_ref.1, bf16[1,128,128]{2,1,0:T(8,128)(2,1)} %v_ref.1, bf16[2048,2048]{1,0:T(8,128)(2,1)} %w_ref.1), custom_call_target="tpu_custom_call" | custom-call | tf_op jit(solution)/shard_map/pallas_call | solution.py:306
  71.8 3.2 %copy.7 = bf16[1,8,64,2048]{3,2,1,0:T(8,128)(2,1)} copy(bf16[1,8,64,2048]{3,2,1,0:T(8,128)(2,1)} %shard_map.55) | data formatting | bytes 4194304
where the time goes:
time: 75.3 us; the launch traced here: 75 us
  Pallas kernels  71.8 us (95%)
  local copies, waits for them, and re-layouts  3.16 us (4%)
    pallas_call x1, Pallas kernels, on_device(): pl.pallas_call(functools.partial(kernel, n_pp, n_cp), out_shape=jax.Shape...  71.8 us
    unnamed x1, local copies, waits for them, and re-layouts  3.16 us

commit v1 on v0

v1 whole, which is shorter than its diff:
```python
import functools

import jax
import jax.numpy as jnp
from jax import lax
from jax.experimental import pallas as pl
from jax.experimental.pallas import tpu as pltpu
from jax.sharding import PartitionSpec as P

HEAD = 128
PARTS = 8
EXTRA = 4
FILL = 3
GIFT = 2
AHEAD = 3
OFF1 = 3
OFF2 = 7
OFF3 = 12
OFFG = 6
SIDE_END = 9
SIDE_MID = 9
LAG_END = 6
LAG_MID = 10
TILES = 4
NEAR = True
MESH = pl.DeviceIdType.MESH


def kernel(
    n_pp,
    n_cp,
    order_ref,
    q_ref,
    k_ref,
    v_ref,
    w_ref,
    out_ref,
    kv,
    qb,
    gs,
    ga,
    wb,
    acc,
    give,
    take,
    mask,
    in_sem,
    qin_sem,
    w_sem,
    kvs_sem,
    kvx_sem,
    kvr_sem,
    qs_sem,
    qg_sem,
    qr_sem,
    y_sem,
    up_sem,
    down_sem,
    x_sem,
    eu_sem,
    ed_sem,
    g_sem,
    ts_sem,
    tr_sem,
):
    pp, cp, tp = lax.axis_index("pp"), lax.axis_index("cp"), lax.axis_index("tp")
    line = n_cp // 2
    i, x = cp // 2, cp % 2
    side = i * 2 + 1 - x
    rows = kv.shape[2]
    half = rows // 2
    width = qb.shape[3]
    wide = wb.shape[1]
    tile = wide // TILES
    heads = width // HEAD
    after, before = lax.rem(pp + 1, n_pp), lax.rem(pp + n_pp - 1, n_pp)
    right = (pp, side, tp)
    sibling = (pp, cp, 1 - tp)
    has_up, has_down = i + 1 < line, i > 0
    end = (i == 0) | (i == line - 1)
    gift_down, gift_up = i == 1, i == line - 2
    giver = jnp.where(i == 0, 1, line - 2) * 2 + x

    def remote(src, dst, send, recv, device):
        return pltpu.make_async_remote_copy(
            src_ref=src,
            dst_ref=dst,
            send_sem=send,
            recv_sem=recv,
            device_id=device,
            device_id_type=MESH,
        )

    load_k = pltpu.make_async_copy(k_ref.at[0], kv.at[cp, 0], in_sem.at[0])
    load_v = pltpu.make_async_copy(v_ref.at[0], kv.at[cp, 1], in_sem.at[1])
    load_k.start()
    load_v.start()

    def load_q(s):
        at = pl.ds(pl.multiple_of(s * width, width), width)
        return pltpu.make_async_copy(q_ref.at[0, :, at], qb.at[0, s], qin_sem.at[s])

    @pl.loop(0, PARTS)
    def _(s):
        load_q(s).start()

    load_w = pltpu.make_async_copy(w_ref, wb, w_sem)
    load_w.start()

    barrier = pltpu.get_barrier_semaphore()

    def greet(device):
        pl.semaphore_signal(barrier, inc=1, device_id=device, device_id_type=MESH)

    @pl.loop(0, line)
    def _(j):
        @pl.when(j != i)
        def _():
            greet((pp, j * 2 + x, tp))

    greet((after, cp, tp))
    greet((before, cp, tp))
    greet(right)
    greet(sibling)
    load_k.wait()
    load_v.wait()
    pl.semaphore_wait(barrier, line + 3)

    def kv_line(j):
        return remote(kv.at[cp], kv.at[cp], kvs_sem.at[j], kvr_sem.at[cp], (pp, j * 2 + x, tp))

    def kv_pass(c):
        return remote(kv.at[c], kv.at[c], kvx_sem.at[c // 2], kvr_sem.at[c], right)

    def q_side(s):
        return remote(qb.at[0, s], qb.at[1, s], qs_sem, qr_sem.at[0, s], right)

    def q_gift(s, to):
        return remote(qb.at[0, s], qb.at[2, s], qg_sem.at[to], qr_sem.at[1, s], (pp, cp - 2 + 4 * to, tp))

    def in_turn(body):
        @pl.loop(0, line - 1)
        def _(e):
            d = e + 1 if NEAR else line - 1 - e
            for j, inside in ((i - d, i - d >= 0), (i + d, i + d < line)):

                @pl.when(inside)
                def _():
                    body(j)

    in_turn(lambda j: kv_line(j).start())
    kv_pass(cp).start()

    @pl.loop(0, PARTS)
    def _(s):
        load_q(s).wait()

        @pl.when(s < FILL)
        def _():
            q_side(s).start()

        for to, there in ((0, gift_down), (1, gift_up)):

            @pl.when(there & (s >= PARTS - GIFT))
            def _():
                q_gift(s, to).start()

    row = lax.broadcasted_iota(jnp.int32, (rows, 1), 0)
    col = lax.broadcasted_iota(jnp.int32, (1, rows), 1)
    for which, block in ((0, cp), (1, side), (2, giver)):
        query_pos = row + jnp.where(row < half, order_ref[2 * block] * half, order_ref[2 * block + 1] * half - half)
        for c in range(n_cp):
            key_pos = col + jnp.where(col < half, order_ref[2 * c] * half, order_ref[2 * c + 1] * half - half)
            mask[which, :, c * rows : (c + 1) * rows] = jnp.where(key_pos <= query_pos, 0.0, -1e30)

    def pass_kv(j):
        kv_pass(j * 2 + x).wait_recv()
        kv_pass(j * 2 + x).start()

    in_turn(pass_kv)

    @pl.loop(FILL, PARTS)
    def _(s):
        q_side(s).start()

    @pl.loop(0, line)
    def _(j):
        kv_pass(j * 2 + 1 - x).wait_recv()

    factor = HEAD ** (-0.5) * 1.4426950408889634
    length = n_cp * rows

    def send_after(which, c, s):
        return remote(gs.at[which, s], ga.at[c, s], y_sem.at[which], g_sem.at[c, s], (after, cp, tp))

    gifts = jnp.where(end, GIFT, 0)

    def attend(a):
        own, gift = a < PARTS, a < PARTS + gifts
        which = jnp.where(own, 0, jnp.where(gift, 2, 1))
        s = a - jnp.where(own, 0, jnp.where(gift, GIFT, PARTS + gifts))

        @pl.when(which == 1)
        def _():
            q_side(s).wait_recv()

        @pl.when(which == 2)
        def _():
            q_gift(s, 0).wait_recv()

        keys = kv[:, 0].reshape(length, HEAD)
        values = kv[:, 1].reshape(length, HEAD)
        for h in range(heads):
            at = slice(h * HEAD, (h + 1) * HEAD)
            score = lax.dot_general(
                qb[which, s, :, at], keys, (((1,), (1,)), ((), ())), preferred_element_type=jnp.float32
            )
            score = score + mask[which]
            weight = jnp.exp2((score - jnp.max(score, axis=1, keepdims=True)) * factor)
            total = jnp.sum(weight, axis=1, keepdims=True)
            mixed = jnp.dot(weight.astype(jnp.bfloat16), values, preferred_element_type=jnp.float32)
            gs[which, s, :, at] = (mixed / total).astype(jnp.bfloat16)
        send_after(which, jnp.where(own, cp, jnp.where(gift, giver, side)), s).start()

    def send_up(c, s):
        return remote(ga.at[c, s], ga.at[c, s], up_sem.at[c // 2], g_sem.at[c, s], (pp, cp + 2, tp))

    def send_down(c, s):
        return remote(ga.at[c, s], ga.at[c, s], down_sem.at[c // 2], g_sem.at[c, s], (pp, cp - 2, tp))

    def send_side(c, s):
        return remote(ga.at[c, s], ga.at[c, s], x_sem.at[c // 2], g_sem.at[c, s], right)

    def extra_up(s):
        return remote(ga.at[side, s], ga.at[side, s], eu_sem, g_sem.at[side, s], (pp, cp + 2, tp))

    def extra_down(s):
        return remote(ga.at[side, s], ga.at[side, s], ed_sem, g_sem.at[side, s], (pp, cp - 2, tp))

    def swap(c):
        return remote(give.at[c], take.at[c], ts_sem.at[c], tr_sem.at[c], sibling)

    def arrived(c, s):
        send_side(c, s).wait_recv()

    def project(c, p):
        for n in range(TILES):
            cols = slice(n * tile, (n + 1) * tile)
            term = None
            for r in range(2):
                at = pl.ds(pl.multiple_of((2 * p + r) * width, width), width)
                piece = jnp.dot(ga[c, 2 * p + r], wb[at, cols], preferred_element_type=jnp.float32)
                term = piece if term is None else term + piece
            acc[c, :, cols] = jnp.where(p == 0, 0.0, acc[c, :, cols]) + term

    def settle(c):
        theirs = pl.ds(pl.multiple_of((1 - tp) * half, half), half)
        give[c] = acc[c, theirs, :].astype(jnp.bfloat16)
        swap(c).start()

    def finish(c):
        ours = pl.ds(pl.multiple_of(tp * half, half), half)
        swap(c).wait_recv()
        out_ref[0, c] = (acc[c, ours, :] + take[c].astype(jnp.float32)).astype(jnp.bfloat16)

    def consume(c, s):
        @pl.when(s % 2 == 1)
        def _():
            project(c, s // 2)

            @pl.when(s == PARTS - 1)
            def _():
                settle(c)

    @pl.loop(0, AHEAD)
    def _(a):
        attend(a)

    load_w.wait()
    lag = jnp.where(end, LAG_END, LAG_MID)
    side_at = jnp.where(end, SIDE_END, SIDE_MID)
    given = PARTS - GIFT

    def passed(d):
        return jnp.where(d == 0, 0, jnp.where(d == 1, OFF1, jnp.where(d == 2, OFF2, OFF3 + (d - 3) * PARTS))) + PARTS

    last_up = jnp.maximum(passed(i), side_at + PARTS) - 1
    last_down = jnp.maximum(passed(line - 1 - i), side_at + PARTS) - 1
    ticks = max(max(OFF2, OFF3 + (line - 4) * PARTS) + max(LAG_END, LAG_MID), SIDE_END, SIDE_MID) + PARTS

    def by_side(d, s):
        return (d > 1) | (s < PARTS - EXTRA)

    def slot(k, tick):
        early = tick < OFF3 + (k % 2) * PARTS
        since = tick - OFF3 - (k % 2) * PARTS
        d = jnp.where(early, 1 + k % 2, 3 + k % 2 + 2 * (since // (2 * PARTS)))
        s = jnp.where(early, tick - jnp.where(k == 0, OFF1, OFF2), lax.rem(since + 2 * PARTS, 2 * PARTS))
        d, s = jnp.where(k == 2, 1, d), jnp.where(k == 2, tick - OFFG, s)
        gift = end & (d == 1) & (s >= given)
        return d, s, (s >= 0) & (s < PARTS) & (d < line) & (gift == (k == 2))

    def places(tick, body):
        @pl.loop(0, 3)
        def _(k):
            d, s, there = slot(k, tick)

            @pl.when(there)
            def _():
                body(d, s)

    @pl.loop(0, ticks)
    def _(tick):
        @pl.when(tick < PARTS)
        def _():
            arrived(cp, tick)

            @pl.when(has_up & ~(gift_up & (tick >= given)))
            def _():
                send_up(cp, tick).start()

            @pl.when(has_down & ~(gift_down & (tick >= given)))
            def _():
                send_down(cp, tick).start()

        def relay(d, s):
            @pl.when(i - d >= 0)
            def _():
                c = cp - 2 * d
                arrived(c, s)

                @pl.when(has_up)
                def _():
                    send_up(c, s).start()

                @pl.when(by_side(d, s))
                def _():
                    send_side(c, s).start()

            @pl.when(i + d < line)
            def _():
                c = cp + 2 * d
                arrived(c, s)

                @pl.when(has_down)
                def _():
                    send_down(c, s).start()

                @pl.when(by_side(d, s))
                def _():
                    send_side(c, s).start()

        places(tick, relay)

        @pl.when(tick + AHEAD < 2 * PARTS + gifts)
        def _():
            attend(tick + AHEAD)

        @pl.when(tick < PARTS)
        def _():
            consume(cp, tick)

        @pl.when((tick >= side_at) & (tick < side_at + PARTS))
        def _():
            arrived(side, tick - side_at)
            consume(side, tick - side_at)

        @pl.when(has_up & (tick == last_up))
        def _():
            @pl.loop(PARTS - EXTRA, PARTS)
            def _(r):
                extra_up(r).start()

        @pl.when(has_down & (tick == last_down))
        def _():
            @pl.loop(PARTS - EXTRA, PARTS)
            def _(r):
                extra_down(r).start()

        def absorb(d, s):
            @pl.loop(0, 2)
            def _(far):
                j = i + (2 * far - 1) * d

                @pl.when((j >= 0) & (j < line))
                def _():
                    consume(j * 2 + x, s)

        places(tick, absorb)

        @pl.when(tick == PARTS + 4)
        def _():
            finish(cp)

        @pl.when(tick == side_at + PARTS - 1)
        def _():
            finish(side)

        for d, at in ((1, max(OFF1, OFFG)), (2, OFF2)):
            if d < line:

                @pl.when(tick == at + PARTS + 3)
                def _():
                    @pl.when(i - d >= 0)
                    def _():
                        finish(cp - 2 * d)

                    @pl.when(i + d < line)
                    def _():
                        finish(cp + 2 * d)

        def absorb_side(d, s):
            @pl.loop(0, 2)
            def _(far):
                j = i + (2 * far - 1) * d

                @pl.when((j >= 0) & (j < line) & by_side(d, s))
                def _():
                    arrived(j * 2 + 1 - x, s)
                    consume(j * 2 + 1 - x, s)

        places(tick - lag, absorb_side)

    @pl.loop(3, line)
    def _(d):
        @pl.when(i - d >= 0)
        def _():
            finish(cp - 2 * d)

        @pl.when(i + d < line)
        def _():
            finish(cp + 2 * d)

    @pl.loop(PARTS - EXTRA, PARTS)
    def _(r):
        @pl.loop(0, 2)
        def _(far):
            j = i + 2 * far - 1

            @pl.when((j >= 0) & (j < line))
            def _():
                arrived(j * 2 + 1 - x, r)
                consume(j * 2 + 1 - x, r)

    @pl.loop(1, line)
    def _(e):
        d = line - e

        @pl.when(i - d >= 0)
        def _():
            finish(side - 2 * d)

        @pl.when(i + d < line)
        def _():
            finish(side + 2 * d)

    in_turn(lambda j: kv_line(j).wait_send())

    def left(ref, sem):
        remote(ref, ref, sem, g_sem.at[0, 0], right).wait_send()

    @pl.loop(0, line)
    def _(j):
        c = j * 2 + x
        kv_pass(c).wait_send()
        near = jnp.abs(j - i) == 1

        @pl.when((j != i) & ~near)
        def _():
            left(ga.at[c], x_sem.at[j])

        @pl.when(near)
        def _():
            left(ga.at[c, 0 : PARTS - EXTRA], x_sem.at[j])

        for there, sem, short in (
            ((j <= i) & has_up, up_sem, gift_up & (j == i)),
            ((j >= i) & has_down, down_sem, gift_down & (j == i)),
        ):

            @pl.when(there & short)
            def _():
                left(ga.at[c, 0:given], sem.at[j])

            @pl.when(there & ~short)
            def _():
                left(ga.at[c], sem.at[j])

    left(qb.at[0], qs_sem)
    left(gs.at[0], y_sem.at[0])
    left(gs.at[1], y_sem.at[1])

    @pl.when(end)
    def _():
        left(gs.at[2, given:PARTS], y_sem.at[2])

    for to, there in ((0, gift_down), (1, gift_up)):

        @pl.when(there)
        def _():
            left(qb.at[0, given:PARTS], qg_sem.at[to])

    @pl.when(has_up)
    def _():
        left(ga.at[side, PARTS - EXTRA : PARTS], eu_sem)

    @pl.when(has_down)
    def _():
        left(ga.at[side, PARTS - EXTRA : PARTS], ed_sem)

    @pl.loop(0, n_cp)
    def _(c):
        swap(c).wait_send()


def on_device(n_pp, n_cp, queries, keys, values, out_weight, span_order):
    rows = queries.shape[1]
    half = rows // 2
    depth, wide = out_weight.shape
    width = depth // PARTS
    line = n_cp // 2
    hbm = pl.BlockSpec(memory_space=pl.ANY)
    dma = pltpu.SemaphoreType.DMA
    queries, keys, values, out_weight, span_order = (
        pltpu.with_memory_space_constraint(a, pltpu.HBM)
        for a in (queries, keys, values, out_weight, span_order)
    )
    return pl.pallas_call(
        functools.partial(kernel, n_pp, n_cp),
        out_shape=pltpu.VMEM((1, n_cp, half, wide), jnp.bfloat16),
        in_specs=[pl.BlockSpec(memory_space=pltpu.SMEM), hbm, hbm, hbm, hbm],
        out_specs=pl.BlockSpec(memory_space=pltpu.VMEM),
        scratch_shapes=[
            pltpu.VMEM((n_cp, 2, rows, HEAD), jnp.bfloat16),
            pltpu.VMEM((3, PARTS, rows, width), jnp.bfloat16),
            pltpu.VMEM((3, PARTS, rows, width), jnp.bfloat16),
            pltpu.VMEM((n_cp, PARTS, rows, width), jnp.bfloat16),
            pltpu.VMEM((depth, wide), jnp.bfloat16),
            pltpu.VMEM((n_cp, rows, wide), jnp.float32),
            pltpu.VMEM((n_cp, half, wide), jnp.bfloat16),
            pltpu.VMEM((n_cp, half, wide), jnp.bfloat16),
            pltpu.VMEM((3, rows, n_cp * rows), jnp.float32),
            dma((2,)),
            dma((PARTS,)),
            dma,
            dma((line,)),
            dma((line,)),
            dma((n_cp,)),
            dma,
            dma((2,)),
            dma((2, PARTS)),
            dma((3,)),
            dma((line,)),
            dma((line,)),
            dma((line,)),
            dma,
            dma,
            dma((n_cp, PARTS)),
            dma((n_cp,)),
            dma((n_cp,)),
        ],
        compiler_params=pltpu.CompilerParams(
            collective_id=0, has_side_effects=True, vmem_limit_bytes=50000 * 1024
        ),
    )(span_order, queries, keys, values, out_weight)


def solution(mesh):
    placed = (P("pp", "cp", "tp"), P("pp", "cp", "tp"), P("pp", "cp", "tp"), P("tp", "cp"), P())
    return jax.shard_map(
        functools.partial(on_device, mesh.shape["pp"], mesh.shape["cp"]),
        mesh=mesh,
        in_specs=placed,
        out_specs=P("pp", None, "tp", "cp"),
        check_vma=False,
    )
```

time: 75.3 us -> 71.8 us (0.954)
  Pallas kernels: 71.8 us -> 69.8 us
  local copies, waits for them, and re-layouts: 3.16 us -> 1.32 us
    pallas_call x1, Pallas kernels: 71.8 us -> 69.8 us  [on_device(): pl.pallas_call(functools.partial(kernel, n_pp, n_cp), out_shape=pltpu.VME...]
    unnamed x1, local copies, waits for them, and re-layouts: 3.16 us -> 1.32 us
where the time goes in v1:
time: 71.8 us; the launch traced here: 71.1 us
  Pallas kernels  69.8 us (97%)
  local copies, waits for them, and re-layouts  1.32 us (2%)
    pallas_call x1, Pallas kernels, on_device(): pl.pallas_call(functools.partial(kernel, n_pp, n_cp), out_shape=pltpu.VME...  69.8 us

profile of v1, /device:TPU:1, one launch (start us, length us, event | category | flops | bytes accessed | tf_op | source)
XLA Modules:
  0.0 71.1 jit_solution(5592340063400211225)
XLA Ops:
  0.0 69.8 %shard_map.55 = bf16[1,8,64,2048]{3,2,1,0:T(8,128)(2,1)S(1)} custom-call(s32[16]{0:T(128)} %order_ref.1, bf16[1,128,2048]{2,1,0:T(8,128)(2,1)} %q_ref.1, bf16[1,128,128]{2,1,0:T(8,128)(2,1)} %k_ref.1, bf16[1,128,128]{2,1,0:T(8,128)(2,1)} %v_ref.1, bf16[2048,2048]{1,0:T(8,128)(2,1)} %w_ref.1), custom_call_target="tpu_custom_call" | custom-call | tf_op jit(solution)/shard_map/pallas_call | solution.py:528
  69.8 1.3 %copy.7 = bf16[1,8,64,2048]{3,2,1,0:T(8,128)(2,1)} copy(bf16[1,8,64,2048]{3,2,1,0:T(8,128)(2,1)S(1)} %shard_map.55) | data formatting | bytes 4194304

commit v2 on v1

--- a/solution.py
+++ b/solution.py
@@ -11,18 +11,20 @@
 PARTS = 8
 EXTRA = 4
 FILL = 3
-GIFT = 2
-AHEAD = 3
+GIFT = 4
+AHEAD = 5
 OFF1 = 3
 OFF2 = 7
-OFF3 = 12
+OFF3 = 13
 OFFG = 6
-SIDE_END = 9
-SIDE_MID = 9
-LAG_END = 6
-LAG_MID = 10
+SIDE_END = 11
+SIDE_MID = 10
+LAG_END = 7
+LAG_MID = 6
 TILES = 4
 NEAR = True
+SPAN = 256
+GROUP = 4
 MESH = pl.DeviceIdType.MESH
 
 
@@ -208,18 +210,37 @@
         def _():
             q_gift(s, 0).wait_recv()
 
-        keys = kv[:, 0].reshape(length, HEAD)
-        values = kv[:, 1].reshape(length, HEAD)
+        blocks = SPAN // rows
+        spans = [(slice(b * blocks, (b + 1) * blocks), slice(b * SPAN, (b + 1) * SPAN)) for b in range(length // SPAN)]
+
+        def scores(h):
+            query = qb[which, s, :, h * HEAD : (h + 1) * HEAD]
+            return [
+                lax.dot_general(
+                    query,
+                    kv[b, 0].reshape(SPAN, HEAD),
+                    (((1,), (1,)), ((), ())),
+                    preferred_element_type=jnp.float32,
+                )
+                + mask[which, :, at]
+                for b, at in spans
+            ]
+
+        ready = scores(0)
         for h in range(heads):
-            at = slice(h * HEAD, (h + 1) * HEAD)
-            score = lax.dot_general(
-                qb[which, s, :, at], keys, (((1,), (1,)), ((), ())), preferred_element_type=jnp.float32
-            )
-            score = score + mask[which]
-            weight = jnp.exp2((score - jnp.max(score, axis=1, keepdims=True)) * factor)
-            total = jnp.sum(weight, axis=1, keepdims=True)
-            mixed = jnp.dot(weight.astype(jnp.bfloat16), values, preferred_element_type=jnp.float32)
-            gs[which, s, :, at] = (mixed / total).astype(jnp.bfloat16)
+            score = ready
+            if h + 1 < heads:
+                ready = scores(h + 1)
+            top = jnp.max(functools.reduce(jnp.maximum, score), axis=1, keepdims=True)
+            weight = [jnp.exp2((z - top) * factor) for z in score]
+            total = jnp.sum(functools.reduce(jnp.add, weight), axis=1, keepdims=True)
+            mixed = None
+            for (b, _), w in zip(spans, weight):
+                term = jnp.dot(
+                    w.astype(jnp.bfloat16), kv[b, 1].reshape(SPAN, HEAD), preferred_element_type=jnp.float32
+                )
+                mixed = term if mixed is None else mixed + term
+            gs[which, s, :, h * HEAD : (h + 1) * HEAD] = (mixed / total).astype(jnp.bfloat16)
         send_after(which, jnp.where(own, cp, jnp.where(gift, giver, side)), s).start()
 
     def send_up(c, s):
@@ -247,9 +268,9 @@
         for n in range(TILES):
             cols = slice(n * tile, (n + 1) * tile)
             term = None
-            for r in range(2):
-                at = pl.ds(pl.multiple_of((2 * p + r) * width, width), width)
-                piece = jnp.dot(ga[c, 2 * p + r], wb[at, cols], preferred_element_type=jnp.float32)
+            for r in range(GROUP):
+                at = pl.ds(pl.multiple_of((GROUP * p + r) * width, width), width)
+                piece = jnp.dot(ga[c, GROUP * p + r], wb[at, cols], preferred_element_type=jnp.float32)
                 term = piece if term is None else term + piece
             acc[c, :, cols] = jnp.where(p == 0, 0.0, acc[c, :, cols]) + term
 
@@ -264,13 +285,14 @@
         out_ref[0, c] = (acc[c, ours, :] + take[c].astype(jnp.float32)).astype(jnp.bfloat16)
 
     def consume(c, s):
-        @pl.when(s % 2 == 1)
-        def _():
-            project(c, s // 2)
-
-            @pl.when(s == PARTS - 1)
-            def _():
-                settle(c)
+        project(c, s // GROUP)
+
+        @pl.when(s == PARTS - 1)
+        def _():
+            settle(c)
+
+    def complete(s):
+        return s % GROUP == GROUP - 1
 
     @pl.loop(0, AHEAD)
     def _(a):
@@ -286,7 +308,7 @@
 
     last_up = jnp.maximum(passed(i), side_at + PARTS) - 1
     last_down = jnp.maximum(passed(line - 1 - i), side_at + PARTS) - 1
-    ticks = max(max(OFF2, OFF3 + (line - 4) * PARTS) + max(LAG_END, LAG_MID), SIDE_END, SIDE_MID) + PARTS
+    ticks = max(max(OFF2, OFF3 + (line - 4) * PARTS) + max(LAG_END, LAG_MID), SIDE_END + 3, SIDE_MID + 3) + PARTS
 
     def by_side(d, s):
         return (d > 1) | (s < PARTS - EXTRA)
@@ -300,15 +322,6 @@
         gift = end & (d == 1) & (s >= given)
         return d, s, (s >= 0) & (s < PARTS) & (d < line) & (gift == (k == 2))
 
-    def places(tick, body):
-        @pl.loop(0, 3)
-        def _(k):
-            d, s, there = slot(k, tick)
-
-            @pl.when(there)
-            def _():
-                body(d, s)
-
     @pl.loop(0, ticks)
     def _(tick):
         @pl.when(tick < PARTS)
@@ -350,20 +363,22 @@
                 def _():
                     send_side(c, s).start()
 
-        places(tick, relay)
+        for k in range(3):
+            d, s, there = slot(k, tick)
+
+            @pl.when(there)
+            def _():
+                relay(d, s)
 
         @pl.when(tick + AHEAD < 2 * PARTS + gifts)
         def _():
             attend(tick + AHEAD)
 
-        @pl.when(tick < PARTS)
-        def _():
-            consume(cp, tick)
-
-        @pl.when((tick >= side_at) & (tick < side_at + PARTS))
-        def _():
-            arrived(side, tick - side_at)
-            consume(side, tick - side_at)
+        beside = tick - side_at
+
+        @pl.when((beside >= 0) & (beside < PARTS))
+        def _():
+            arrived(side, beside)
 
         @pl.when(has_up & (tick == last_up))
         def _():
@@ -377,22 +392,11 @@
             def _(r):
                 extra_down(r).start()
 
-        def absorb(d, s):
-            @pl.loop(0, 2)
-            def _(far):
-                j = i + (2 * far - 1) * d
-
-                @pl.when((j >= 0) & (j < line))
-                def _():
-                    consume(j * 2 + x, s)
-
-        places(tick, absorb)
-
         @pl.when(tick == PARTS + 4)
         def _():
             finish(cp)
 
-        @pl.when(tick == side_at + PARTS - 1)
+        @pl.when(tick == side_at + PARTS + 2)
         def _():
             finish(side)
 
@@ -409,17 +413,33 @@
                     def _():
                         finish(cp + 2 * d)
 
-        def absorb_side(d, s):
-            @pl.loop(0, 2)
-            def _(far):
-                j = i + (2 * far - 1) * d
-
-                @pl.when((j >= 0) & (j < line) & by_side(d, s))
-                def _():
-                    arrived(j * 2 + 1 - x, s)
-                    consume(j * 2 + 1 - x, s)
-
-        places(tick - lag, absorb_side)
+        @pl.loop(0, 8)
+        def _(k):
+            over = k // 4
+            place = k % 4
+            d, s, there = slot(place, tick - over * lag)
+            home = jnp.where(over == 1, beside, tick)
+            d, s = jnp.where(place == 3, 0, d), jnp.where(place == 3, home, s)
+            there = jnp.where(place == 3, ((home >= 0) & (home < PARTS)).astype(jnp.int32), there.astype(jnp.int32))
+            column = jnp.where(over == 1, 1 - x, x)
+            apart = (over == 1) & (d > 0)
+
+            @pl.when((there == 1) & complete(s) & (~apart | by_side(d, s)))
+            def _():
+                @pl.loop(jnp.where(d == 0, 1, 0), 2)
+                def _(far):
+                    j = i + (2 * far - 1) * d
+                    c = j * 2 + column
+
+                    @pl.when((j >= 0) & (j < line))
+                    def _():
+                        @pl.when(apart)
+                        def _():
+                            @pl.loop(0, GROUP)
+                            def _(r):
+                                arrived(c, s - (GROUP - 1) + r)
+
+                        consume(c, s)
 
     @pl.loop(3, line)
     def _(d):
@@ -440,7 +460,10 @@
             @pl.when((j >= 0) & (j < line))
             def _():
                 arrived(j * 2 + 1 - x, r)
-                consume(j * 2 + 1 - x, r)
+
+                @pl.when(complete(r))
+                def _():
+                    consume(j * 2 + 1 - x, r)
 
     @pl.loop(1, line)
     def _(e):

time: 71.8 us -> 67.1 us (0.935)
  Pallas kernels: 69.8 us -> 65.7 us
    pallas_call x1, Pallas kernels: 69.8 us -> 65.7 us  [on_device(): pl.pallas_call(functools.partial(kernel, n_pp, n_cp), out_shape=pltpu.VME...]
where the time goes in v2:
time: 67.1 us; the launch traced here: 67 us
  Pallas kernels  65.7 us (98%)
  local copies, waits for them, and re-layouts  1.32 us (2%)
    pallas_call x1, Pallas kernels, on_device(): pl.pallas_call(functools.partial(kernel, n_pp, n_cp), out_shape=pltpu.VME...  65.7 us

profile of v2, /device:TPU:1, one launch (start us, length us, event | category | flops | bytes accessed | tf_op | source)
XLA Modules:
  0.0 67.0 jit_solution(8747644318435947634)
XLA Ops:
  0.0 65.7 %shard_map.55 = bf16[1,8,64,2048]{3,2,1,0:T(8,128)(2,1)S(1)} custom-call(s32[16]{0:T(128)} %order_ref.1, bf16[1,128,2048]{2,1,0:T(8,128)(2,1)} %q_ref.1, bf16[1,128,128]{2,1,0:T(8,128)(2,1)} %k_ref.1, bf16[1,128,128]{2,1,0:T(8,128)(2,1)} %v_ref.1, bf16[2048,2048]{1,0:T(8,128)(2,1)} %w_ref.1), custom_call_target="tpu_custom_call" | custom-call | tf_op jit(solution)/shard_map/pallas_call | solution.py:551
  65.7 1.3 %copy.7 = bf16[1,8,64,2048]{3,2,1,0:T(8,128)(2,1)} copy(bf16[1,8,64,2048]{3,2,1,0:T(8,128)(2,1)S(1)} %shard_map.55) | data formatting | bytes 4194304

commit v3 on v2

--- a/solution.py
+++ b/solution.py
@@ -12,14 +12,14 @@
 EXTRA = 4
 FILL = 3
 GIFT = 4
-AHEAD = 5
+AHEAD = 6
 OFF1 = 3
 OFF2 = 7
 OFF3 = 13
 OFFG = 6
 SIDE_END = 11
 SIDE_MID = 10
-LAG_END = 7
+LAG_END = 5
 LAG_MID = 6
 TILES = 4
 NEAR = True
@@ -31,12 +31,13 @@
 def kernel(
     n_pp,
     n_cp,
-    order_ref,
+    order_in,
     q_ref,
     k_ref,
     v_ref,
     w_ref,
     out_ref,
+    order_ref,
     kv,
     qb,
     gs,
@@ -47,6 +48,7 @@
     take,
     mask,
     in_sem,
+    order_sem,
     qin_sem,
     w_sem,
     kvs_sem,
@@ -95,8 +97,10 @@
 
     load_k = pltpu.make_async_copy(k_ref.at[0], kv.at[cp, 0], in_sem.at[0])
     load_v = pltpu.make_async_copy(v_ref.at[0], kv.at[cp, 1], in_sem.at[1])
+    load_order = pltpu.make_async_copy(order_in, order_ref, order_sem)
     load_k.start()
     load_v.start()
+    load_order.start()
 
     def load_q(s):
         at = pl.ds(pl.multiple_of(s * width, width), width)
@@ -128,11 +132,11 @@
     load_v.wait()
     pl.semaphore_wait(barrier, line + 3)
 
-    def kv_line(j):
-        return remote(kv.at[cp], kv.at[cp], kvs_sem.at[j], kvr_sem.at[cp], (pp, j * 2 + x, tp))
-
-    def kv_pass(c):
-        return remote(kv.at[c], kv.at[c], kvx_sem.at[c // 2], kvr_sem.at[c], right)
+    def kv_line(j, r):
+        return remote(kv.at[cp, r], kv.at[cp, r], kvs_sem.at[j, r], kvr_sem.at[cp, r], (pp, j * 2 + x, tp))
+
+    def kv_pass(c, r):
+        return remote(kv.at[c, r], kv.at[c, r], kvx_sem.at[c // 2, r], kvr_sem.at[c, r], right)
 
     def q_side(s):
         return remote(qb.at[0, s], qb.at[1, s], qs_sem, qr_sem.at[0, s], right)
@@ -150,8 +154,13 @@
                 def _():
                     body(j)
 
-    in_turn(lambda j: kv_line(j).start())
-    kv_pass(cp).start()
+    @in_turn
+    def _(j):
+        for r in range(2):
+            kv_line(j, r).start()
+
+    for r in range(2):
+        kv_pass(cp, r).start()
 
     @pl.loop(0, PARTS)
     def _(s):
@@ -167,6 +176,7 @@
             def _():
                 q_gift(s, to).start()
 
+    load_order.wait()
     row = lax.broadcasted_iota(jnp.int32, (rows, 1), 0)
     col = lax.broadcasted_iota(jnp.int32, (1, rows), 1)
     for which, block in ((0, cp), (1, side), (2, giver)):
@@ -176,8 +186,9 @@
             mask[which, :, c * rows : (c + 1) * rows] = jnp.where(key_pos <= query_pos, 0.0, -1e30)
 
     def pass_kv(j):
-        kv_pass(j * 2 + x).wait_recv()
-        kv_pass(j * 2 + x).start()
+        for r in range(2):
+            kv_pass(j * 2 + x, r).wait_recv()
+            kv_pass(j * 2 + x, r).start()
 
     in_turn(pass_kv)
 
@@ -187,7 +198,8 @@
 
     @pl.loop(0, line)
     def _(j):
-        kv_pass(j * 2 + 1 - x).wait_recv()
+        for r in range(2):
+            kv_pass(j * 2 + 1 - x, r).wait_recv()
 
     factor = HEAD ** (-0.5) * 1.4426950408889634
     length = n_cp * rows
@@ -292,7 +304,7 @@
             settle(c)
 
     def complete(s):
-        return s % GROUP == GROUP - 1
+        return (s & (GROUP - 1)) == GROUP - 1
 
     @pl.loop(0, AHEAD)
     def _(a):
@@ -314,13 +326,21 @@
         return (d > 1) | (s < PARTS - EXTRA)
 
     def slot(k, tick):
-        early = tick < OFF3 + (k % 2) * PARTS
-        since = tick - OFF3 - (k % 2) * PARTS
-        d = jnp.where(early, 1 + k % 2, 3 + k % 2 + 2 * (since // (2 * PARTS)))
-        s = jnp.where(early, tick - jnp.where(k == 0, OFF1, OFF2), lax.rem(since + 2 * PARTS, 2 * PARTS))
-        d, s = jnp.where(k == 2, 1, d), jnp.where(k == 2, tick - OFFG, s)
-        gift = end & (d == 1) & (s >= given)
-        return d, s, (s >= 0) & (s < PARTS) & (d < line) & (gift == (k == 2))
+        if k == 2:
+            s = tick - OFFG
+            return 1, s, end & (s >= given) & (s < PARTS) & (line > 1)
+        since = tick - OFF3 - k * PARTS
+        later = since >= 0
+        turn = since // (2 * PARTS)
+        d = jnp.where(later, 3 + k + 2 * turn, 1 + k)
+        s = jnp.where(later, since - turn * (2 * PARTS), tick - (OFF1, OFF2)[k])
+        there = (s >= 0) & (s < PARTS) & (d < line)
+        if k == 0:
+            there &= ~(end & (d == 1) & (s >= given))
+        return d, s, there
+
+    def left(ref, sem):
+        remote(ref, ref, sem, g_sem.at[0, 0], right).wait_send()
 
     @pl.loop(0, ticks)
     def _(tick):
@@ -363,8 +383,8 @@
                 def _():
                     send_side(c, s).start()
 
-        for k in range(3):
-            d, s, there = slot(k, tick)
+        here = [slot(k, tick) for k in range(3)]
+        for d, s, there in here:
 
             @pl.when(there)
             def _():
@@ -392,100 +412,139 @@
             def _(r):
                 extra_down(r).start()
 
-        @pl.when(tick == PARTS + 4)
-        def _():
-            finish(cp)
-
-        @pl.when(tick == side_at + PARTS + 2)
-        def _():
-            finish(side)
-
-        for d, at in ((1, max(OFF1, OFFG)), (2, OFF2)):
-            if d < line:
-
-                @pl.when(tick == at + PARTS + 3)
-                def _():
-                    @pl.when(i - d >= 0)
+        marks = [PARTS + 4, side_at + PARTS + 2, max(OFF1, OFFG) + PARTS + 3, OFF2 + PARTS + 3]
+
+        @pl.when(functools.reduce(jnp.logical_or, [tick == mark for mark in marks]))
+        def _():
+            @pl.when(tick == PARTS + 4)
+            def _():
+                finish(cp)
+
+            @pl.when(tick == side_at + PARTS + 2)
+            def _():
+                finish(side)
+
+            for d, at in ((1, max(OFF1, OFFG)), (2, OFF2)):
+                if d < line:
+
+                    @pl.when(tick == at + PARTS + 3)
                     def _():
-                        finish(cp - 2 * d)
-
-                    @pl.when(i + d < line)
-                    def _():
-                        finish(cp + 2 * d)
-
-        @pl.loop(0, 8)
-        def _(k):
-            over = k // 4
-            place = k % 4
-            d, s, there = slot(place, tick - over * lag)
-            home = jnp.where(over == 1, beside, tick)
-            d, s = jnp.where(place == 3, 0, d), jnp.where(place == 3, home, s)
-            there = jnp.where(place == 3, ((home >= 0) & (home < PARTS)).astype(jnp.int32), there.astype(jnp.int32))
-            column = jnp.where(over == 1, 1 - x, x)
-            apart = (over == 1) & (d > 0)
-
-            @pl.when((there == 1) & complete(s) & (~apart | by_side(d, s)))
-            def _():
-                @pl.loop(jnp.where(d == 0, 1, 0), 2)
+                        @pl.when(i - d >= 0)
+                        def _():
+                            finish(cp - 2 * d)
+
+                        @pl.when(i + d < line)
+                        def _():
+                            finish(cp + 2 * d)
+
+        @pl.when(tick == ticks - 1)
+        def _():
+            @pl.loop(2, line)
+            def _(d):
+                @pl.when((i - d >= 0) & (d > 2))
+                def _():
+                    finish(cp - 2 * d)
+
+                @pl.when((i + d < line) & (d > 2))
+                def _():
+                    finish(cp + 2 * d)
+
+                @pl.when((i - d >= 0) & (d < line - 1))
+                def _():
+                    finish(side - 2 * d)
+
+                @pl.when((i + d < line) & (d < line - 1))
+                def _():
+                    finish(side + 2 * d)
+
+            @in_turn
+            def _(j):
+                for r in range(2):
+                    kv_line(j, r).wait_send()
+
+            @pl.loop(0, line)
+            def _(j):
+                for r in range(2):
+                    kv_pass(j * 2 + x, r).wait_send()
+
+            left(qb.at[0], qs_sem)
+            left(gs.at[0], y_sem.at[0])
+            left(gs.at[1], y_sem.at[1])
+
+            @pl.when(end)
+            def _():
+                left(gs.at[2, given:PARTS], y_sem.at[2])
+
+            for to, there in ((0, gift_down), (1, gift_up)):
+
+                @pl.when(there)
+                def _():
+                    left(qb.at[0, given:PARTS], qg_sem.at[to])
+
+            @pl.loop(PARTS - EXTRA, PARTS)
+            def _(r):
+                @pl.loop(0, 2)
                 def _(far):
-                    j = i + (2 * far - 1) * d
-                    c = j * 2 + column
+                    j = i + 2 * far - 1
 
                     @pl.when((j >= 0) & (j < line))
                     def _():
-                        @pl.when(apart)
+                        arrived(j * 2 + 1 - x, r)
+
+                        @pl.when(complete(r))
                         def _():
-                            @pl.loop(0, GROUP)
-                            def _(r):
-                                arrived(c, s - (GROUP - 1) + r)
-
-                        consume(c, s)
-
-    @pl.loop(3, line)
-    def _(d):
+                            consume(j * 2 + 1 - x, r)
+
+        past = [slot(k, tick - lag) for k in range(3)]
+        items = [(0, *item) for item in here] + [(0, 0, tick, tick < PARTS)]
+        items += [(1, d, s, there & by_side(d, s)) for d, s, there in past]
+        items += [(1, 0, beside, (beside >= 0) & (beside < PARTS))]
+        due = [there & complete(s) for _, _, s, there in items]
+
+        @pl.when(functools.reduce(jnp.logical_or, due))
+        def _():
+            @pl.loop(0, len(items))
+            def _(k):
+                def pick(values):
+                    chosen = values[0]
+                    for n, value in enumerate(values[1:], 1):
+                        chosen = jnp.where(k == n, value, chosen)
+                    return chosen
+
+                @pl.when(pick([flag.astype(jnp.int32) for flag in due]) == 1)
+                def _():
+                    over = k // 4
+                    d, s = pick([item[1] for item in items]), pick([item[2] for item in items])
+                    column = jnp.where(over == 1, 1 - x, x)
+
+                    @pl.loop(jnp.where(d == 0, 1, 0), 2)
+                    def _(far):
+                        j = i + (2 * far - 1) * d
+                        c = j * 2 + column
+
+                        @pl.when((j >= 0) & (j < line))
+                        def _():
+                            @pl.when((over == 1) & (d > 0))
+                            def _():
+                                @pl.loop(0, GROUP)
+                                def _(r):
+                                    arrived(c, s - (GROUP - 1) + r)
+
+                            consume(c, s)
+
+    for d in sorted({line - 1, 1}, reverse=True):
+
         @pl.when(i - d >= 0)
         def _():
-            finish(cp - 2 * d)
+            finish(side - 2 * d)
 
         @pl.when(i + d < line)
         def _():
-            finish(cp + 2 * d)
-
-    @pl.loop(PARTS - EXTRA, PARTS)
-    def _(r):
-        @pl.loop(0, 2)
-        def _(far):
-            j = i + 2 * far - 1
-
-            @pl.when((j >= 0) & (j < line))
-            def _():
-                arrived(j * 2 + 1 - x, r)
-
-                @pl.when(complete(r))
-                def _():
-                    consume(j * 2 + 1 - x, r)
-
-    @pl.loop(1, line)
-    def _(e):
-        d = line - e
-
-        @pl.when(i - d >= 0)
-        def _():
-            finish(side - 2 * d)
-
-        @pl.when(i + d < line)
-        def _():
             finish(side + 2 * d)
-
-    in_turn(lambda j: kv_line(j).wait_send())
-
-    def left(ref, sem):
-        remote(ref, ref, sem, g_sem.at[0, 0], right).wait_send()
 
     @pl.loop(0, line)
     def _(j):
         c = j * 2 + x
-        kv_pass(c).wait_send()
         near = jnp.abs(j - i) == 1
 
         @pl.when((j != i) & ~near)
@@ -508,20 +567,6 @@
             @pl.when(there & ~short)
             def _():
                 left(ga.at[c], sem.at[j])
-
-    left(qb.at[0], qs_sem)
-    left(gs.at[0], y_sem.at[0])
-    left(gs.at[1], y_sem.at[1])
-
-    @pl.when(end)
-    def _():
-        left(gs.at[2, given:PARTS], y_sem.at[2])
-
-    for to, there in ((0, gift_down), (1, gift_up)):
-
-        @pl.when(there)
-        def _():
-            left(qb.at[0, given:PARTS], qg_sem.at[to])
 
     @pl.when(has_up)
     def _():
@@ -551,9 +596,10 @@
     return pl.pallas_call(
         functools.partial(kernel, n_pp, n_cp),
         out_shape=pltpu.VMEM((1, n_cp, half, wide), jnp.bfloat16),
-        in_specs=[pl.BlockSpec(memory_space=pltpu.SMEM), hbm, hbm, hbm, hbm],
+        in_specs=[hbm] * 5,
         out_specs=pl.BlockSpec(memory_space=pltpu.VMEM),
         scratch_shapes=[
+            pltpu.SMEM(span_order.shape, jnp.int32),
             pltpu.VMEM((n_cp, 2, rows, HEAD), jnp.bfloat16),
             pltpu.VMEM((3, PARTS, rows, width), jnp.bfloat16),
             pltpu.VMEM((3, PARTS, rows, width), jnp.bfloat16),
@@ -564,11 +610,12 @@
             pltpu.VMEM((n_cp, half, wide), jnp.bfloat16),
             pltpu.VMEM((3, rows, n_cp * rows), jnp.float32),
             dma((2,)),
+            dma,
             dma((PARTS,)),
             dma,
-            dma((line,)),
-            dma((line,)),
-            dma((n_cp,)),
+            dma((line, 2)),
+            dma((line, 2)),
+            dma((n_cp, 2)),
             dma,
             dma((2,)),
             dma((2, PARTS)),

time: 67.1 us -> 62.3 us (0.928)
  Pallas kernels: 65.7 us -> 60.8 us
    pallas_call x1, Pallas kernels: 65.7 us -> 60.8 us  [on_device(): pl.pallas_call(functools.partial(kernel, n_pp, n_cp), out_shape=pltpu.VME...]
where the time goes in v3:
time: 62.3 us; the launch traced here: 62.1 us
  Pallas kernels  60.8 us (98%)
  local copies, waits for them, and re-layouts  1.32 us (2%)
    pallas_call x1, Pallas kernels, on_device(): pl.pallas_call(functools.partial(kernel, n_pp, n_cp), out_shape=pltpu.VME...  60.8 us
    unnamed x1, local copies, waits for them, and re-layouts  1.32 us

profile of v3, /device:TPU:1, one launch (start us, length us, event | category | flops | bytes accessed | tf_op | source)
XLA Modules:
  0.0 62.1 jit_solution(4832871077951149503)
XLA Ops:
  0.0 60.8 %shard_map.55 = bf16[1,8,64,2048]{3,2,1,0:T(8,128)(2,1)S(1)} custom-call(s32[16]{0:T(128)} %order_in.1, bf16[1,128,2048]{2,1,0:T(8,128)(2,1)} %q_ref.1, bf16[1,128,128]{2,1,0:T(8,128)(2,1)} %k_ref.1, bf16[1,128,128]{2,1,0:T(8,128)(2,1)} %v_ref.1, bf16[2048,2048]{1,0:T(8,128)(2,1)} %w_ref.1), custom_call_target="tpu_custom_call" | custom-call | tf_op jit(solution)/shard_map/pallas_call | solution.py:596
  60.8 1.3 %copy.7 = bf16[1,8,64,2048]{3,2,1,0:T(8,128)(2,1)} copy(bf16[1,8,64,2048]{3,2,1,0:T(8,128)(2,1)S(1)} %shard_map.55) | data formatting | bytes 4194304

commit v4 on v3

--- a/solution.py
+++ b/solution.py
@@ -10,7 +10,7 @@
 HEAD = 128
 PARTS = 8
 EXTRA = 4
-FILL = 3
+FILL = 1
 GIFT = 4
 AHEAD = 6
 OFF1 = 3
@@ -170,12 +170,6 @@
         def _():
             q_side(s).start()
 
-        for to, there in ((0, gift_down), (1, gift_up)):
-
-            @pl.when(there & (s >= PARTS - GIFT))
-            def _():
-                q_gift(s, to).start()
-
     load_order.wait()
     row = lax.broadcasted_iota(jnp.int32, (rows, 1), 0)
     col = lax.broadcasted_iota(jnp.int32, (1, rows), 1)
@@ -191,6 +185,14 @@
             kv_pass(j * 2 + x, r).start()
 
     in_turn(pass_kv)
+
+    for to, there in ((0, gift_down), (1, gift_up)):
+
+        @pl.when(there)
+        def _():
+            @pl.loop(PARTS - GIFT, PARTS)
+            def _(s):
+                q_gift(s, to).start()
 
     @pl.loop(FILL, PARTS)
     def _(s):

time: 62.3 us -> 60.5 us (0.971)
  Pallas kernels: 60.8 us -> 59 us
    pallas_call x1, Pallas kernels: 60.8 us -> 59 us  [on_device(): pl.pallas_call(functools.partial(kernel, n_pp, n_cp), out_shape=pltpu.VME...]
where the time goes in v4:
time: 60.5 us; the launch traced here: 60.3 us
  Pallas kernels  59 us (98%)
  local copies, waits for them, and re-layouts  1.32 us (2%)
    pallas_call x1, Pallas kernels, on_device(): pl.pallas_call(functools.partial(kernel, n_pp, n_cp), out_shape=pltpu.VME...  59 us
    unnamed x1, local copies, waits for them, and re-layouts  1.32 us

profile of v4, /device:TPU:1, one launch (start us, length us, event | category | flops | bytes accessed | tf_op | source)
XLA Modules:
  0.0 60.3 jit_solution(10639452234143554558)
XLA Ops:
  0.0 59.0 %shard_map.55 = bf16[1,8,64,2048]{3,2,1,0:T(8,128)(2,1)S(1)} custom-call(s32[16]{0:T(128)} %order_in.1, bf16[1,128,2048]{2,1,0:T(8,128)(2,1)} %q_ref.1, bf16[1,128,128]{2,1,0:T(8,128)(2,1)} %k_ref.1, bf16[1,128,128]{2,1,0:T(8,128)(2,1)} %v_ref.1, bf16[2048,2048]{1,0:T(8,128)(2,1)} %w_ref.1), custom_call_target="tpu_custom_call" | custom-call | tf_op jit(solution)/shard_map/pallas_call | solution.py:598
  59.0 1.3 %copy.7 = bf16[1,8,64,2048]{3,2,1,0:T(8,128)(2,1)} copy(bf16[1,8,64,2048]{3,2,1,0:T(8,128)(2,1)S(1)} %shard_map.55) | data formatting | bytes 4194304

commit v5 on v4

--- a/solution.py
+++ b/solution.py
@@ -21,7 +21,7 @@
 SIDE_MID = 10
 LAG_END = 5
 LAG_MID = 6
-TILES = 4
+TILES = 8
 NEAR = True
 SPAN = 256
 GROUP = 4
@@ -364,26 +364,26 @@
                 c = cp - 2 * d
                 arrived(c, s)
 
+                @pl.when(by_side(d, s))
+                def _():
+                    send_side(c, s).start()
+
                 @pl.when(has_up)
                 def _():
                     send_up(c, s).start()
-
-                @pl.when(by_side(d, s))
-                def _():
-                    send_side(c, s).start()
 
             @pl.when(i + d < line)
             def _():
                 c = cp + 2 * d
                 arrived(c, s)
 
+                @pl.when(by_side(d, s))
+                def _():
+                    send_side(c, s).start()
+
                 @pl.when(has_down)
                 def _():
                     send_down(c, s).start()
-
-                @pl.when(by_side(d, s))
-                def _():
-                    send_side(c, s).start()
 
         here = [slot(k, tick) for k in range(3)]
         for d, s, there in here:

time: 60.5 us -> 60.5 us (level)
  no operation moved by 1% of the time
where the time goes in v5:
time: 60.5 us; the launch traced here: 60.3 us
  Pallas kernels  59 us (98%)
  local copies, waits for them, and re-layouts  1.32 us (2%)
    pallas_call x1, Pallas kernels, on_device(): pl.pallas_call(functools.partial(kernel, n_pp, n_cp), out_shape=pltpu.VME...  59 us
    unnamed x1, local copies, waits for them, and re-layouts  1.32 us

profile of v5, /device:TPU:1, one launch (start us, length us, event | category | flops | bytes accessed | tf_op | source)
XLA Modules:
  0.0 60.3 jit_solution(9953753857586343759)
XLA Ops:
  0.0 59.0 %shard_map.55 = bf16[1,8,64,2048]{3,2,1,0:T(8,128)(2,1)S(1)} custom-call(s32[16]{0:T(128)} %order_in.1, bf16[1,128,2048]{2,1,0:T(8,128)(2,1)} %q_ref.1, bf16[1,128,128]{2,1,0:T(8,128)(2,1)} %k_ref.1, bf16[1,128,128]{2,1,0:T(8,128)(2,1)} %v_ref.1, bf16[2048,2048]{1,0:T(8,128)(2,1)} %w_ref.1), custom_call_target="tpu_custom_call" | custom-call | tf_op jit(solution)/shard_map/pallas_call | solution.py:598
  59.0 1.3 %copy.7 = bf16[1,8,64,2048]{3,2,1,0:T(8,128)(2,1)} copy(bf16[1,8,64,2048]{3,2,1,0:T(8,128)(2,1)S(1)} %shard_map.55) | data formatting | bytes 4194304
